TPU v7x, 32 devices: a whole 2x2x4 slice. The times are simulated.
32 devices in a mesh: groups: 2 (over x), ep: 4 (over y, core), rep: 4 (over z).
Axes of the slice: x: 2, y: 2, z: 4, core: 2. Of those that a mesh axis runs over, the one named last changes fastest.
Arguments:
- prompt_hidden: bfloat16 [8, 96, 2048], P('groups', 'ep'), parts along dimension 0, may hold values from -6 to 6
- decode_hidden: bfloat16 [64, 8, 2048], P(('groups', 'ep'), 'rep'), parts along dimension 0, may hold values from -6 to 6
- queries: bfloat16 [64, 8, 2048], P(('groups', 'ep'), None, 'rep'), parts along dimension 0, may hold values from -128 to 128
- attn_gain: float32 [2048], replicated, may hold values from 0.1 to 1.9
- key_value_weight: bfloat16 [2048, 1024], P(None, 'rep'), may hold values from -0.125 to 0.125
- out_weight: bfloat16 [2048, 2048], P('rep'), may hold values from -0.5 to 0.5
- moe_gain: float32 [2048], replicated, may hold values from 0.1 to 1.9
- gate_weight: bfloat16 [16, 2048, 768], P(('ep', 'rep')), may hold values from -0.125 to 0.125
- up_weight: bfloat16 [16, 2048, 768], P(('ep', 'rep')), may hold values from -0.125 to 0.125
- down_weight: bfloat16 [16, 768, 2048], P(('ep', 'rep')), may hold values from -0.21875 to 0.21875
- expert_table: int32 [151936], replicated, may hold values from 0 to 15, as said below
- token_ids: int32 [32, 8], P('ep', 'rep'), may hold values from 0 to 151935, as said below
- prompt_lengths: int32 [8], P('groups'), parts along dimension 0, may hold values from 1 to 96, 240 in all
Outputs:
- layer_out: bfloat16 [64, 8, 2048], P(('groups', 'ep'), 'rep'), parts along dimension 0
There are 2 independent parts, one for each index of `groups`. A program takes and returns all parts, laid end to end along the dimension named above; an argument that names none is the same for every part. Nothing has to cross between parts.
Inputs may be any that keep to these rules, and one draw needn't show every extreme that they name: `expert_table`: each expert is the value of exactly 9496 entries. `token_ids`: a device holds the 8 sequences of its index of ep at 8 // 4 steps of its index of rep; of these tokens at most 2 go to one expert; in every draw one expert receives exactly 2 from every device. `prompt_lengths`: the lengths of a group sum to 240 and the longest is 96.
All inputs are finite; a program needn't handle non-finite values.
Results may differ from a plain program's by a relative error of at most 0.017.
The roundings to bfloat16 on the way count: a program that leaves them out, or rounds other values in their place, can miss the bound.
Values may be sent and summed in bfloat16 or wider, within the bound.
No kernel may reach another device: no remote copies, remote signals or barrier semaphores. Data moves between devices by JAX's collectives and lax.ppermute only.
A program may use at most 128 MiB of HBM per device.

v0:
```python
import math
import jax
import jax.numpy as jnp
from jax import lax
from jax.sharding import PartitionSpec as P

HEAD_DIM = 128
QUERY_HEADS = 16
KEY_VALUE_HEADS = 4
GROUP_PROMPTS = 4
CAP = 2
EPS = 1e-06
THETA = 1000000.0


def swapped(block, axis, bit):
    count = lax.axis_size(axis)
    route = []
    for low in range(count):
        high = low | 1 << bit
        if high != low and high < count:
            route += [(low, high), (high, low)]
    return lax.ppermute(block, axis, route)


def rms_scale(hidden, gain_vec):
    widened = hidden.astype(jnp.float32)
    mean_sq = jnp.mean(widened * widened, axis=-1, keepdims=True)
    return widened * lax.rsqrt(mean_sq + EPS) * gain_vec


def rotate(vectors, positions):
    half_dim = vectors.shape[-1] // 2
    inverse_freq = jnp.exp(
        jnp.arange(half_dim, dtype=jnp.float32) * (-2.0 * math.log(THETA) / vectors.shape[-1])
    )
    angles = positions[..., None] * inverse_freq
    cosine = jnp.cos(angles)
    sine_part = jnp.sin(angles)
    first_half = vectors[..., :half_dim]
    second_half = vectors[..., half_dim:]
    return jnp.concatenate(
        [
            first_half * cosine - second_half * sine_part,
            second_half * cosine + first_half * sine_part,
        ],
        axis=-1,
    )


def expert_apply(tokens, gate_weight, up_weight, down_weight):
    flat_rows = tokens.reshape(-1, tokens.shape[-1])
    gate_proj = jnp.dot(flat_rows, gate_weight[0], preferred_element_type=jnp.float32)
    up_proj = jnp.dot(flat_rows, up_weight[0], preferred_element_type=jnp.float32)
    hidden = (jax.nn.silu(gate_proj) * up_proj).astype(jnp.bfloat16)
    return (
        jnp.dot(hidden, down_weight[0], preferred_element_type=jnp.float32)
        .astype(jnp.bfloat16)
        .reshape(tokens.shape)
    )


def local(
    prompt_hidden,
    decode_hidden,
    queries,
    attn_gain,
    key_value_weight,
    out_weight,
    moe_gain,
    gate_weight,
    up_weight,
    down_weight,
    expert_table,
    token_ids,
    prompt_lengths,
):
    full_hidden = lax.all_gather(decode_hidden, "rep", axis=1, tiled=True)
    sequences_local, steps_total, model_width = full_hidden.shape
    prompt_length_local = prompt_hidden.shape[1]
    qh_dev = queries.shape[2] // HEAD_DIM
    group_count = QUERY_HEADS // KEY_VALUE_HEADS
    ep_count = lax.axis_size("ep")
    rep_count = lax.axis_size("rep")
    ep_index = lax.axis_index("ep")
    rep_index = lax.axis_index("rep")
    seq_total = sequences_local * ep_count
    samples = seq_total // GROUP_PROMPTS
    score_scale = HEAD_DIM ** (-0.5)
    step_rows = steps_total // rep_count
    blocks = key_value_weight.shape[1] // HEAD_DIM

    def own_columns(hidden, positions):
        leading = hidden.shape[:-1]
        normed = rms_scale(hidden, attn_gain).astype(jnp.bfloat16)
        projected = jnp.dot(
            normed.reshape(-1, model_width), key_value_weight, preferred_element_type=jnp.float32
        )
        projected = projected.reshape(leading + (blocks, HEAD_DIM))
        block_ids = rep_index * blocks + jnp.arange(blocks, dtype=jnp.int32)
        is_key = (block_ids % 2 == 0)[:, None]
        turned = rotate(projected, positions[..., None])
        return (
            jnp.where(is_key, turned, projected)
            .astype(jnp.bfloat16)
            .reshape(leading + (blocks * HEAD_DIM,))
        )

    key_pos = ep_index * prompt_length_local + jnp.arange(prompt_length_local, dtype=jnp.int32)
    prompt_pos = jnp.broadcast_to(
        key_pos.astype(jnp.float32)[None, :], (GROUP_PROMPTS, prompt_length_local)
    )
    own_seqs = ep_index * sequences_local + jnp.arange(sequences_local, dtype=jnp.int32)
    own_prompt = own_seqs // samples
    own_lengths = jnp.take(prompt_lengths, own_prompt)
    decode_pos = (
        own_lengths[:, None].astype(jnp.float32)
        + jnp.arange(steps_total, dtype=jnp.float32)[None, :]
    )
    prompt_part = own_columns(prompt_hidden, prompt_pos)
    decode_part = own_columns(full_hidden, decode_pos)
    prompt_hot = own_prompt[:, None] == jnp.arange(GROUP_PROMPTS, dtype=jnp.int32)[None, :]
    if blocks == 1:
        partner_prompt, partner_decode = swapped((prompt_part, decode_part), "rep", 0)
        holds_key = rep_index % 2 == 0
        prompt_columns = jnp.where(
            holds_key,
            jnp.concatenate([prompt_part, partner_prompt], axis=2),
            jnp.concatenate([partner_prompt, prompt_part], axis=2),
        )
        decode_columns = jnp.where(
            holds_key,
            jnp.concatenate([decode_part, partner_decode], axis=2),
            jnp.concatenate([partner_decode, decode_part], axis=2),
        )
        heads_here = 1
        head_base = rep_index // 2
    else:
        prompt_columns = prompt_part
        decode_columns = decode_part
        heads_here = blocks // 2
        head_base = rep_index * heads_here
    prompt_key_value = prompt_columns.reshape(
        GROUP_PROMPTS, prompt_length_local, heads_here, 2, HEAD_DIM
    )
    decode_key_value = decode_columns.reshape(sequences_local, steps_total, heads_here, 2, HEAD_DIM)
    prompt_keys = prompt_key_value[:, :, :, 0, :]
    prompt_values = prompt_key_value[:, :, :, 1, :]
    decode_keys = decode_key_value[:, :, :, 0, :]
    decode_values = decode_key_value[:, :, :, 1, :]
    query_matrix = queries.reshape(sequences_local, steps_total, qh_dev, HEAD_DIM)
    head_pick = (
        rep_index * qh_dev + jnp.arange(qh_dev, dtype=jnp.int32)
    ) // group_count - head_base
    own_keys = jnp.take(decode_keys, head_pick, axis=2)
    own_values = jnp.take(decode_values, head_pick, axis=2)
    self_scores = (
        jnp.einsum("sthd,suhd->sthu", query_matrix, own_keys, preferred_element_type=jnp.float32)
        * score_scale
    )
    self_mask = (
        jnp.arange(steps_total, dtype=jnp.int32)[None, :]
        <= jnp.arange(steps_total, dtype=jnp.int32)[:, None]
    )[None, :, None, :]
    self_scores = jnp.where(self_mask, self_scores, -1e30)
    self_top = jnp.max(self_scores, axis=-1)
    start_weights = jnp.where(self_mask, jnp.exp(self_scores - self_top[..., None]), 0.0)
    row_top = self_top
    row_total = jnp.sum(start_weights, axis=-1)
    weighted = jnp.einsum(
        "sthu,suhd->sthd",
        start_weights.astype(jnp.bfloat16),
        own_values,
        preferred_element_type=jnp.float32,
    )
    piece_keys = jnp.take(lax.all_gather(prompt_keys, "ep", axis=1, tiled=True), head_pick, axis=2)
    piece_values = jnp.take(
        lax.all_gather(prompt_values, "ep", axis=1, tiled=True), head_pick, axis=2
    )
    piece_len = piece_keys.shape[1]
    valid = jnp.arange(piece_len, dtype=jnp.int32)[None, :] < prompt_lengths[:, None]
    key_mask = prompt_hot[:, None, None, :, None] & valid[None, None, None, :, :]
    scores = (
        jnp.einsum("sthd,pnhd->sthpn", query_matrix, piece_keys, preferred_element_type=jnp.float32)
        * score_scale
    )
    scores = jnp.where(key_mask, scores, -1e30)
    new_top = jnp.maximum(row_top, jnp.max(scores, axis=(-2, -1)))
    decay = jnp.exp(row_top - new_top)
    weights = jnp.where(key_mask, jnp.exp(scores - new_top[..., None, None]), 0.0)
    weighted = weighted * decay[..., None] + jnp.einsum(
        "sthpn,pnhd->sthd",
        weights.astype(jnp.bfloat16),
        piece_values,
        preferred_element_type=jnp.float32,
    )
    row_top, row_total, weighted = (
        new_top,
        row_total * decay + jnp.sum(weights, axis=(-2, -1)),
        weighted,
    )
    attended = weighted / row_total[..., None]
    heads_out = attended.reshape(sequences_local, steps_total, qh_dev * HEAD_DIM).astype(
        jnp.bfloat16
    )
    by_step = jnp.swapaxes(heads_out, 0, 1)
    attn_sum = jnp.swapaxes(
        lax.psum_scatter(
            jnp.dot(
                by_step.reshape(-1, by_step.shape[-1]),
                out_weight,
                preferred_element_type=jnp.float32,
            )
            .reshape(step_rows * lax.axis_size("rep"), sequences_local, model_width)
            .astype(jnp.bfloat16),
            "rep",
            scatter_dimension=0,
            tiled=True,
        ).astype(jnp.float32),
        0,
        1,
    )
    attn_mixed = (decode_hidden.astype(jnp.float32) + attn_sum).astype(jnp.bfloat16)
    row_count = sequences_local * step_rows
    normed = rms_scale(attn_mixed, moe_gain).astype(jnp.bfloat16).reshape(row_count, model_width)
    chosen = jnp.take(expert_table, token_ids.reshape(row_count))
    device_count = ep_count * rep_count
    slot_total = device_count * CAP
    same_expert = chosen[:, None] == chosen[None, :]
    before = jnp.arange(row_count)[None, :] < jnp.arange(row_count)[:, None]
    slot_rank = jnp.sum((same_expert & before).astype(jnp.int32), axis=1)
    destination = chosen * CAP + slot_rank
    send_pick = (jnp.arange(slot_total, dtype=jnp.int32)[:, None] == destination[None, :]).astype(
        jnp.bfloat16
    )
    outgoing = (
        jnp.dot(send_pick, normed, preferred_element_type=jnp.float32)
        .astype(jnp.bfloat16)
        .reshape(device_count, CAP, model_width)
    )
    served = expert_apply(
        lax.all_to_all(outgoing, ("ep", "rep"), split_axis=0, concat_axis=0, tiled=True),
        gate_weight,
        up_weight,
        down_weight,
    )
    returned = lax.all_to_all(served, ("ep", "rep"), split_axis=0, concat_axis=0, tiled=True)
    moe_out = lax.dot_general(
        send_pick,
        returned.reshape(slot_total, model_width),
        (((0,), (0,)), ((), ())),
        preferred_element_type=jnp.float32,
    )
    layer_out = (
        attn_mixed.astype(jnp.float32) + moe_out.reshape(sequences_local, step_rows, model_width)
    ).astype(jnp.bfloat16)
    return layer_out


def solution(mesh):
    placed = (
        P("groups", "ep", None),
        P(("groups", "ep"), "rep", None),
        P(("groups", "ep"), None, "rep"),
        P(),
        P(None, "rep"),
        P("rep", None),
        P(),
        P(("ep", "rep"), None, None),
        P(("ep", "rep"), None, None),
        P(("ep", "rep"), None, None),
        P(),
        P("ep", "rep"),
        P("groups"),
    )
    return jax.shard_map(
        local,
        mesh=mesh,
        in_specs=placed,
        out_specs=P(("groups", "ep"), "rep", None),
        check_vma=False,
    )
```

profile of v0, /device:TPU:0, one launch (start us, length us, event | category | flops | bytes accessed | tf_op | source)
XLA Modules:
  0.0 108.6 jit_solution(1051078798896082952)
XLA Ops:
  6.5 0.0 copy-start
  6.5 0.0 copy-start.4
  6.5 0.0 reduce-scatter.2.cloned.1.call-start
  6.6 0.9 iota_compare_fusion.5
  7.5 1.3 %gather_fusion = s32[8]{0:T(128)S(1)} fusion(s32[4]{0:T(128)} %param.29, s32[1024]{0:T(1024)S(1)} %pad_clamp_fusion.1), kind=kCustom, calls=%fused_computation | custom fusion | bytes 96 | tf_op jit(solution)/shard_map/jit(_take)/gather | solution.py:115
  8.8 2.3 %copy.120 = bf16[256,2048]{1,0:T(8,128)(2,1)} copy(bf16[256,2048]{0,1:T(8,128)(2,1)} %bitcast.124) | data formatting | bytes 2097152 | tf_op jit(solution)/shard_map/dot_general | solution.py:96
  11.1 0.0 copy-start.7
  11.1 0.9 copy.92
  12.0 15.7 %all_gather.9 = bf16[8,8,2048]{2,0,1:T(8,128)(2,1)S(1)} all-gather(bf16[8,2,2048]{2,0,1:T(8,128)(2,1)S(1)} %copy.92), channel_id=1, replica_groups=mesh['groups'=2,'ep'=4,'rep'=4] {'rep'}, dimensions={1}, use_global_device_ids=true | all-gather | bytes 327680 | tf_op jit(solution)/shard_map/all_gather | solution.py:78
  27.7 0.1 fusion.31
  27.9 0.2 multiply_cosine_fusion.1
  28.1 0.0 copy-done.4
  28.1 1.7 %fusion.48 = f32[8,8,2,128]{3,0,2,1:T(8,128)S(1)} fusion(bf16[2,128,2048,1]{2,1,0,3:T(8,128)(2,1)} %bitcast.122, bf16[8,8,2048]{2,0,1:T(8,128)(2,1)S(1)} %all_gather.9, f32[2048]{0:T(1024)S(1)} %copy-done.4, f32[8,8]{0,1:T(8,128)S(1)} %add_rsqrt_fusion), kind=kOutput, calls=%fused_computation.53 | convolution fusion | flops 67633152 | bytes 1384704 | tf_op jit(solution)/shard_map/dot_general | solution.py:96
  29.7 0.1 multiply_subtract_fusion.1
  29.8 0.1 fusion.83
  30.0 0.1 multiply_cosine_fusion
  30.1 1.1 %fusion.28 = f32[4,24]{1,0:T(4,128)S(1)} fusion(bf16[4,24,2048]{2,1,0:T(8,128)(2,1)} %param.17), kind=kLoop, calls=%fused_computation.31 | loop fusion | flops 589728 | bytes 393600 | tf_op jit(solution)/shard_map/reduce_sum | solution.py:28
  31.3 1.8 %fusion.37 = f32[4,24,2,128]{3,1,2,0:T(8,128)S(1)} fusion(bf16[2,128,2048,1]{2,1,0,3:T(8,128)(2,1)} %bitcast.123, bf16[4,24,2048]{2,1,0:T(8,128)(2,1)} %param.17, f32[2048]{0:T(1024)S(1)} %copy-done.4, f32[4,24]{1,0:T(4,128)S(1)} %add_rsqrt_fusion.1), kind=kOutput, calls=%fused_computation.43 | convolution fusion | flops 101449728 | bytes 1548672 | tf_op jit(solution)/shard_map/dot_general | solution.py:96
  33.1 0.0 copy-start.1
  33.1 0.1 multiply_subtract_fusion
  33.2 0.1 fusion.81
  33.4 5.5 %all-gather = bf16[4,96,1,1,128]{4,1,3,0,2:T(8,128)(2,1)S(1)} all-gather(bf16[4,24,1,1,128]{4,1,3,0,2:T(8,128)(2,1)S(1)} %get-tuple-element.16), channel_id=2, replica_groups=mesh['groups'=2,'ep'=4,'rep'=4] {'ep'}, dimensions={1}, use_global_device_ids=true | all-gather | bytes 122880 | tf_op jit(solution)/shard_map/all_gather | solution.py:176
  38.8 0.0 copy-done.7
  38.8 0.3 fusion.105
  39.1 0.1 fusion.61
  39.2 0.1 broadcast_and_fusion
  39.3 0.6 fusion.104
  39.8 0.0 copy-start.6
  39.8 0.3 fusion.34
  40.1 0.0 copy-start.2
  40.1 0.0 copy-start.5
  40.2 5.3 %all-gather.1 = bf16[4,96,1,1,128]{4,1,3,0,2:T(8,128)(2,1)S(1)} all-gather(bf16[4,24,1,1,128]{4,1,3,0,2:T(8,128)(2,1)S(1)} %get-tuple-element.15), channel_id=3, replica_groups=mesh['groups'=2,'ep'=4,'rep'=4] {'ep'}, dimensions={1}, use_global_device_ids=true | all-gather | bytes 122880 | tf_op jit(solution)/shard_map/all_gather | solution.py:178
  45.5 0.3 convolution_bitcast_fusion
  45.8 0.3 fusion.25
  46.1 0.0 copy-done.1
  46.1 1.2 %convolution_convert_fusion = bf16[8,8,2048]{2,1,0:T(8,128)(2,1)} fusion(bf16[512,2048]{1,0:T(8,128)(2,1)S(1)} %copy-done.1, bf16[8,8,512]{2,0,1:T(8,128)(2,1)S(1)} %fusion.25), kind=kOutput, calls=%fused_computation.8 | convolution fusion | flops 134348800 | bytes 2424832 | tf_op jit(solution)/shard_map/dot_general | solution.py:209
  47.3 0.0 reduce-scatter.2.cloned.1.call-update
  47.3 0.0 copy-done.6
  47.3 0.1 copy.107
  47.4 0.1 reshape.383
  47.5 0.1 reshape.382
  47.6 1.5 %gather_fusion.1 = s32[16]{0:T(128)S(1)} fusion(s32[151936]{0:T(1024)} %param.27, s32[1024]{0:T(1024)S(1)} %pad_clamp_fusion), kind=kCustom, calls=%fused_computation.1 | custom fusion | bytes 192 | tf_op jit(solution)/shard_map/jit(_take)/gather | solution.py:226
  49.1 0.2 convert_reduce_fusion
  49.2 19.7 %reduce-scatter.2.cloned.1.call-done = bf16[2,8,2048]{2,1,0:T(8,128)(2,1)} async-done(((bf16[8,8,2048]{2,1,0:T(8,128)(2,1)}), bf16[2,8,2048]{2,1,0:T(8,128)(2,1)}) %reduce-scatter.2.cloned.1.call-update) | async-done | bytes 65552 | tf_op jit(solution)/shard_map/reduce_scatter | solution.py:208
  69.0 0.0 copy-done.2
  69.0 1.0 fusion.57
  70.0 0.0 copy-done.5
  70.0 0.9 fusion.59
  70.9 0.1 copy.109
  71.0 0.2 convolution_convert_fusion.1
  71.2 0.1 reshape.385
  71.3 10.7 %all_to_all.10 = bf16[16,2,2048]{2,1,0:T(2,128)(2,1)} all-to-all(bf16[16,2,2048]{2,1,0:T(2,128)(2,1)S(1)} %reshape.385), channel_id=1, replica_groups=mesh['groups'=2,'ep'=4,'rep'=4] {'ep','rep'}, dimensions={0} | all-to-all | bytes 262144 | tf_op jit(solution)/shard_map/all_to_all | solution.py:242
  81.9 1.0 reshape.386
  82.9 3.1 %fusion.4 = f32[32,768]{1,0:T(8,128)} fusion(bf16[32,2048]{1,0:T(8,128)(2,1)S(1)} %reshape.386, bf16[1,2048,768]{2,1,0:T(8,128)(2,1)} %param.24), kind=kOutput, calls=%fused_computation.6 | convolution fusion | flops 100663296 | bytes 3375104 | tf_op jit(solution)/shard_map/dot_general | solution.py:53
  86.0 0.0 copy-done
  86.0 3.2 %fusion.6 = bf16[32,2048]{1,0:T(8,128)(2,1)S(1)} fusion(bf16[1,768,2048]{2,1,0:T(8,128)(2,1)S(1)} %copy-done, bf16[32,2048]{1,0:T(8,128)(2,1)S(1)} %reshape.386, bf16[1,2048,768]{2,1,0:T(8,128)(2,1)} %param.25, f32[32,768]{1,0:T(8,128)} %fusion.4), kind=kOutput, calls=%fused_computation.9 | convolution fusion | flops 201539584 | bytes 6651904 | tf_op jit(solution)/shard_map/dot_general | solution.py:57
  89.2 0.8 reshape.387
  90.0 3.5 %all-to-all-start.1 = ((bf16[16,2,2048]{2,1,0:T(2,128)(2,1)}), bf16[16,2,2048]{2,1,0:T(2,128)(2,1)S(1)}, u32[]{:S(2)}, u32[]{:S(2)}) async-start(bf16[16,2,2048]{2,1,0:T(2,128)(2,1)} %reshape.387), calls=%async_computation.2 | async-start | bytes 262144 | tf_op jit(solution)/shard_map/all_to_all | solution.py:247
  93.5 0.1 iota_compare_fusion.3
  93.6 7.3 %all-to-all-done.1 = bf16[16,2,2048]{2,1,0:T(2,128)(2,1)S(1)} async-done(((bf16[16,2,2048]{2,1,0:T(2,128)(2,1)}), bf16[16,2,2048]{2,1,0:T(2,128)(2,1)S(1)}, u32[]{:S(2)}, u32[]{:S(2)}) %all-to-all-start.1) | async-done | bytes 131104 | tf_op jit(solution)/shard_map/all_to_all | solution.py:247
  100.9 0.1 reshape.424
  100.9 0.0 copy-done.3
  100.9 0.1 fusion.9
  101.1 0.7 copy.111
  (28 shorter events, 0.2 us)
Async XLA Ops:
  6.5 79.5 %copy-start = (bf16[1,768,2048]{2,1,0:T(8,128)(2,1)S(1)}, bf16[1,768,2048]{2,1,0:T(8,128)(2,1)}, u32[]{:S(2)}) copy-start(bf16[1,768,2048]{2,1,0:T(8,128)(2,1)} %param.26) | copy-start | bytes 9437188
  6.5 21.5 %copy-start.4 = (f32[2048]{0:T(1024)S(1)}, f32[2048]{0:T(1024)}, u32[]{:S(2)}) copy-start(f32[2048]{0:T(1024)} %param.20) | copy-start | bytes 24580
  6.5 62.4 %reduce-scatter.2.cloned.1.call-start = ((), (), s32[]{:S(2)}) async-start(), calls=%async_computation.3 | async-start | bytes 327680 | tf_op jit(solution)/shard_map/reduce_scatter | solution.py:208
  11.1 27.7 %copy-start.7 = (bf16[8,8,512]{2,1,0:T(8,128)(2,1)S(1)}, bf16[8,8,512]{2,1,0:T(8,128)(2,1)}, u32[]{:S(2)}) copy-start(bf16[8,8,512]{2,1,0:T(8,128)(2,1)} %param.19) | copy-start | bytes 196612
  33.1 12.9 %copy-start.1 = (bf16[512,2048]{1,0:T(8,128)(2,1)S(1)}, bf16[512,2048]{1,0:T(8,128)(2,1)}, u32[]{:S(2)}) copy-start(bf16[512,2048]{1,0:T(8,128)(2,1)} %param.22) | copy-start | bytes 6291460
  39.8 7.5 %copy-start.6 = (s32[8,2]{0,1:T(2,128)S(1)}, s32[8,2]{0,1:T(2,128)}, u32[]{:S(2)}) copy-start(s32[8,2]{0,1:T(2,128)} %param.28) | copy-start | bytes 196
  40.1 28.9 %copy-start.2 = (bf16[8,2,2048]{2,1,0:T(2,128)(2,1)S(1)}, bf16[8,2,2048]{2,1,0:T(2,128)(2,1)}, u32[]{:S(2)}) copy-start(bf16[8,2,2048]{2,1,0:T(2,128)(2,1)} %param.18) | copy-start | bytes 196612
  40.1 29.8 %copy-start.5 = (f32[2048]{0:T(1024)S(1)}, f32[2048]{0:T(1024)}, u32[]{:S(2)}) copy-start(f32[2048]{0:T(1024)} %param.23) | copy-start | bytes 24580
  86.0 14.9 %copy-start.3 = (bf16[2,8,2048]{2,1,0:T(8,128)(2,1)S(1)}, bf16[2,8,2048]{2,1,0:T(8,128)(2,1)}, u32[]{:S(2)}) copy-start(bf16[2,8,2048]{2,1,0:T(8,128)(2,1)} %reduce-scatter.2.cloned.1.call-done) | copy-start | bytes 196612
  90.0 10.9 %all-to-all-start.1 = ((bf16[16,2,2048]{2,1,0:T(2,128)(2,1)}), bf16[16,2,2048]{2,1,0:T(2,128)(2,1)S(1)}, u32[]{:S(2)}, u32[]{:S(2)}) async-start(bf16[16,2,2048]{2,1,0:T(2,128)(2,1)} %reshape.387), calls=%async_computation.2 | async-start | bytes 262144 | tf_op jit(solution)/shard_map/all_to_all | solution.py:247
Sparse Core Ops, SparseCore 0:
  47.4 21.5 reduce-scatter.1
where the time goes:
time: 109 us
  blocking collectives  37.1 us (34%)
  waiting for transfers between devices  27 us (25%)
  between operations  13.7 us (13%)
  matrix products  12.7 us (12%)
  local copies, waits for them, and re-layouts  9 us (8%)
  other arithmetic  5.59 us (5%)
  starting transfers between devices  3.51 us (3%)
    reduce_scatter x1, waiting for transfers between devices, local(): lax.psum_scatter(jnp.dot(by_step.reshape(-1, by_step.shape[-1]), out_weig...  19.7 us
    all_gather x1, blocking collectives, local(): full_hidden = lax.all_gather(decode_hidden, 'rep', axis=1, tiled=True)  15.7 us
    all_to_all x1, blocking collectives, local(): lax.all_to_all(outgoing, ('ep', 'rep'), split_axis=0, concat_axis=0, tile...  10.7 us
    all_to_all x1, waiting for transfers between devices, local(): lax.all_to_all(served, ('ep', 'rep'), split_axis=0, concat_axis=0, tiled=...  7.26 us
    all_gather x1, blocking collectives, local(): lax.all_gather(prompt_keys, 'ep', axis=1, tiled=True)  5.46 us
    all_gather x1, blocking collectives, local(): lax.all_gather(prompt_values, 'ep', axis=1, tiled=True)  5.33 us
    all_to_all x1, starting transfers between devices, local(): lax.all_to_all(served, ('ep', 'rep'), split_axis=0, concat_axis=0, tiled=...  3.51 us
    dot_general x2, matrix products, own_columns(): jnp.dot(normed.reshape(-1, model_width), key_value_weight, preferred_elem...  3.51 us
  transfers between devices with their start and end apart: 2, of which 2 were waited for; matrix products, arithmetic and copies ran while one was open for 2% of the time, Pallas kernels for 0%

commit v1 on v0

--- a/solution.py
+++ b/solution.py
@@ -11,6 +11,18 @@
 CAP = 2
 EPS = 1e-06
 THETA = 1000000.0
+
+
+def rotated_exchange(value, axis, split, join):
+    ways, here = (lax.axis_size(axis), lax.axis_index(axis))
+    width = value.shape[split] // ways
+    turned = jnp.roll(value, -here * width, axis=split)
+    got = [lax.slice_in_dim(turned, 0, width, axis=split)]
+    for far in range(1, ways):
+        sent = lax.slice_in_dim(turned, far * width, (far + 1) * width, axis=split)
+        got.append(lax.ppermute(sent, axis, [(d, (d + far) % ways) for d in range(ways)]))
+    line = jnp.concatenate(got[::-1], axis=join)
+    return jnp.roll(line, (here + 1) * got[0].shape[join], axis=join)
 
 
 def swapped(block, axis, bit):
@@ -239,10 +251,7 @@
         .reshape(device_count, CAP, model_width)
     )
     served = expert_apply(
-        lax.all_to_all(outgoing, ("ep", "rep"), split_axis=0, concat_axis=0, tiled=True),
-        gate_weight,
-        up_weight,
-        down_weight,
+        rotated_exchange(outgoing, ("ep", "rep"), 0, 0), gate_weight, up_weight, down_weight
     )
     returned = lax.all_to_all(served, ("ep", "rep"), split_axis=0, concat_axis=0, tiled=True)
     moe_out = lax.dot_general(

time: 109 us -> 122 us (1.12)
  starting transfers between devices: 3.51 us -> 21.7 us
  blocking collectives: 37.1 us -> 26.4 us
  waiting for transfers between devices: 27 us -> 32.5 us
    ppermute x0 -> x15, starting transfers between devices: none -> 18.1 us  [rotated_exchange(): lax.ppermute(sent, axis, [(d, (d + far) % ways) for d in range(ways)])]
    all_to_all x1 -> x0, blocking collectives: 10.7 us -> none  [local(): lax.all_to_all(outgoing, ('ep', 'rep'), split_axis=0, concat_axis=0, tile...]
    ppermute x0 -> x15, waiting for transfers between devices: none -> 5.56 us  [rotated_exchange(): lax.ppermute(sent, axis, [(d, (d + far) % ways) for d in range(ways)])]
  transfers between devices with their start and end apart: 2 -> 17, of which waited for: 2 -> 6; matrix products, arithmetic and copies ran while one was open for 2% -> 2% of each run, Pallas kernels for 0% -> 0%
where the time goes in v1:
time: 122 us
  waiting for transfers between devices  32.5 us (27%)
  blocking collectives  26.4 us (22%)
  starting transfers between devices  21.7 us (18%)
  between operations  13.9 us (11%)
  matrix products  12.7 us (10%)
  local copies, waits for them, and re-layouts  8.4 us (7%)
  other arithmetic  6.29 us (5%)
    reduce_scatter x1, waiting for transfers between devices, local(): lax.psum_scatter(jnp.dot(by_step.reshape(-1, by_step.shape[-1]), out_weig...  19.7 us
    ppermute x15, starting transfers between devices, rotated_exchange(): lax.ppermute(sent, axis, [(d, (d + far) % ways) for d in range(ways)])  18.1 us
    all_gather x1, blocking collectives, local(): full_hidden = lax.all_gather(decode_hidden, 'rep', axis=1, tiled=True)  15.7 us
    all_to_all x1, waiting for transfers between devices, local(): lax.all_to_all(served, ('ep', 'rep'), split_axis=0, concat_axis=0, tiled=...  7.26 us
    ppermute x15, waiting for transfers between devices, rotated_exchange(): lax.ppermute(sent, axis, [(d, (d + far) % ways) for d in range(ways)])  5.56 us
    all_gather x1, blocking collectives, local(): lax.all_gather(prompt_keys, 'ep', axis=1, tiled=True)  5.46 us
    all_gather x1, blocking collectives, local(): lax.all_gather(prompt_values, 'ep', axis=1, tiled=True)  5.33 us
    all_to_all x1, starting transfers between devices, local(): lax.all_to_all(served, ('ep', 'rep'), split_axis=0, concat_axis=0, tiled=...  3.51 us
  transfers between devices with their start and end apart: 17, of which 6 were waited for; matrix products, arithmetic and copies ran while one was open for 2% of the time, Pallas kernels for 0%

profile of v1, /device:TPU:0, one launch (start us, length us, event | category | flops | bytes accessed | tf_op | source)
XLA Modules:
  0.0 121.9 jit_solution(8094455138869729478)
XLA Ops:
  6.6 0.9 iota_compare_fusion.5
  7.5 1.3 %gather_fusion = s32[8]{0:T(128)S(1)} fusion(s32[4]{0:T(128)} %param.31, s32[1024]{0:T(1024)S(1)} %pad_clamp_fusion.1), kind=kCustom, calls=%fused_computation | custom fusion | bytes 96 | tf_op jit(solution)/shard_map/jit(_take)/gather | solution.py:127
  8.8 2.3 %copy.120 = bf16[256,2048]{1,0:T(8,128)(2,1)} copy(bf16[256,2048]{0,1:T(8,128)(2,1)} %bitcast.124) | data formatting | bytes 2097152 | tf_op jit(solution)/shard_map/dot_general | solution.py:108
  11.1 0.9 copy.92
  12.0 15.7 %all_gather.9 = bf16[8,8,2048]{2,0,1:T(8,128)(2,1)S(1)} all-gather(bf16[8,2,2048]{2,0,1:T(8,128)(2,1)S(1)} %copy.92), channel_id=1, replica_groups=mesh['groups'=2,'ep'=4,'rep'=4] {'rep'}, dimensions={1}, use_global_device_ids=true | all-gather | bytes 327680 | tf_op jit(solution)/shard_map/all_gather | solution.py:90
  27.7 0.1 fusion.31
  27.8 0.2 multiply_cosine_fusion.1
  28.0 1.7 %fusion.48 = f32[8,8,2,128]{3,0,2,1:T(8,128)S(1)} fusion(bf16[2,128,2048,1]{2,1,0,3:T(8,128)(2,1)} %bitcast.122, bf16[8,8,2048]{2,0,1:T(8,128)(2,1)S(1)} %all_gather.9, f32[2048]{0:T(1024)S(1)} %copy-done.4, f32[8,8]{0,1:T(8,128)S(1)} %add_rsqrt_fusion), kind=kOutput, calls=%fused_computation.53 | convolution fusion | flops 67633152 | bytes 1384704 | tf_op jit(solution)/shard_map/dot_general | solution.py:108
  29.7 0.1 multiply_subtract_fusion.1
  29.8 0.1 fusion.85
  30.0 0.1 multiply_cosine_fusion
  30.1 1.1 fusion.28
  31.3 1.8 %fusion.37 = f32[4,24,2,128]{3,1,2,0:T(8,128)S(1)} fusion(bf16[2,128,2048,1]{2,1,0,3:T(8,128)(2,1)} %bitcast.123, bf16[4,24,2048]{2,1,0:T(8,128)(2,1)} %param.19, f32[2048]{0:T(1024)S(1)} %copy-done.4, f32[4,24]{1,0:T(4,128)S(1)} %add_rsqrt_fusion.1), kind=kOutput, calls=%fused_computation.43 | convolution fusion | flops 101449728 | bytes 1548672 | tf_op jit(solution)/shard_map/dot_general | solution.py:108
  33.1 0.1 multiply_subtract_fusion
  33.2 0.1 fusion.83
  33.3 5.5 %all-gather = bf16[4,96,1,1,128]{4,1,3,0,2:T(8,128)(2,1)S(1)} all-gather(bf16[4,24,1,1,128]{4,1,3,0,2:T(8,128)(2,1)S(1)} %get-tuple-element.32), channel_id=2, replica_groups=mesh['groups'=2,'ep'=4,'rep'=4] {'ep'}, dimensions={1}, use_global_device_ids=true | all-gather | bytes 122880 | tf_op jit(solution)/shard_map/all_gather | solution.py:188
  38.8 0.1 broadcast_and_fusion
  38.9 0.3 fusion.108
  39.2 0.6 fusion.107
  39.7 0.1 fusion.63
  39.8 0.3 fusion.34
  40.2 5.3 %all-gather.1 = bf16[4,96,1,1,128]{4,1,3,0,2:T(8,128)(2,1)S(1)} all-gather(bf16[4,24,1,1,128]{4,1,3,0,2:T(8,128)(2,1)S(1)} %get-tuple-element.31), channel_id=3, replica_groups=mesh['groups'=2,'ep'=4,'rep'=4] {'ep'}, dimensions={1}, use_global_device_ids=true | all-gather | bytes 122880 | tf_op jit(solution)/shard_map/all_gather | solution.py:190
  45.5 0.3 convolution_bitcast_fusion
  45.8 0.3 fusion.25
  46.1 1.2 convolution_convert_fusion
  47.3 0.1 copy.107
  47.4 0.1 reshape.383
  47.4 0.1 reshape.382
  47.6 1.5 %gather_fusion.1 = s32[16]{0:T(128)S(1)} fusion(s32[151936]{0:T(1024)} %param.29, s32[1024]{0:T(1024)S(1)} %pad_clamp_fusion), kind=kCustom, calls=%fused_computation.1 | custom fusion | bytes 192 | tf_op jit(solution)/shard_map/jit(_take)/gather | solution.py:238
  49.1 0.2 convert_reduce_fusion
  49.3 19.7 %reduce-scatter.2.cloned.1.call-done = bf16[2,8,2048]{2,1,0:T(8,128)(2,1)} async-done(((bf16[8,8,2048]{2,1,0:T(8,128)(2,1)}), bf16[2,8,2048]{2,1,0:T(8,128)(2,1)}) %reduce-scatter.2.cloned.1.call-update) | async-done | bytes 65552 | tf_op jit(solution)/shard_map/reduce_scatter | solution.py:220
  68.9 1.0 fusion.59
  69.9 0.9 fusion.61
  70.8 0.1 copy.109
  71.0 0.2 convolution_convert_fusion.1
  71.1 0.1 reshape.385
  71.2 0.3 fusion.58
  71.6 0.1 fusion.105
  71.8 0.1 collective-permute-start.1
  71.9 3.2 %collective-permute-start.2 = (bf16[1,2,2048]{2,1,0:T(2,128)(2,1)S(1)}, bf16[1,2,2048]{2,1,0:T(2,128)(2,1)S(1)}, u32[]{:S(2)}, u32[]{:S(2)}) collective-permute-start(bf16[1,2,2048]{2,1,0:T(2,128)(2,1)S(1)} %get-tuple-element.26), channel_id=1, source_target_pairs={{0,13},{1,14},{2,15},{3,0},{4,1},{5,2},{6,3},{7,4},{8,5},{9,6},{10... | collective-permute-start | bytes 24584 | tf_op jit(solution)/shard_map/ppermute | solution.py:23
  75.1 2.2 %collective-permute-start.4 = (bf16[1,2,2048]{2,1,0:T(2,128)(2,1)S(1)}, bf16[1,2,2048]{2,1,0:T(2,128)(2,1)S(1)}, u32[]{:S(2)}, u32[]{:S(2)}) collective-permute-start(bf16[1,2,2048]{2,1,0:T(2,128)(2,1)S(1)} %get-tuple-element.24), channel_id=1, source_target_pairs={{0,11},{1,12},{2,13},{3,14},{4,15},{5,0},{6,1},{7,2},{8,3},{9,4},{... | collective-permute-start | bytes 24584 | tf_op jit(solution)/shard_map/ppermute | solution.py:23
  77.2 1.3 %collective-permute-start.5 = (bf16[1,2,2048]{2,1,0:T(2,128)(2,1)S(1)}, bf16[1,2,2048]{2,1,0:T(2,128)(2,1)S(1)}, u32[]{:S(2)}, u32[]{:S(2)}) collective-permute-start(bf16[1,2,2048]{2,1,0:T(2,128)(2,1)S(1)} %get-tuple-element.23), channel_id=1, source_target_pairs={{0,10},{1,11},{2,12},{3,13},{4,14},{5,15},{6,0},{7,1},{8,2},{9,3},... | collective-permute-start | bytes 24584 | tf_op jit(solution)/shard_map/ppermute | solution.py:23
  78.5 1.8 %collective-permute-start.6 = (bf16[1,2,2048]{2,1,0:T(2,128)(2,1)S(1)}, bf16[1,2,2048]{2,1,0:T(2,128)(2,1)S(1)}, u32[]{:S(2)}, u32[]{:S(2)}) collective-permute-start(bf16[1,2,2048]{2,1,0:T(2,128)(2,1)S(1)} %get-tuple-element.22), channel_id=1, source_target_pairs={{0,9},{1,10},{2,11},{3,12},{4,13},{5,14},{6,15},{7,0},{8,1},{9,2},... | collective-permute-start | bytes 24584 | tf_op jit(solution)/shard_map/ppermute | solution.py:23
  80.4 0.6 collective-permute-start.7
  81.0 1.9 %collective-permute-start.8 = (bf16[1,2,2048]{2,1,0:T(2,128)(2,1)S(1)}, bf16[1,2,2048]{2,1,0:T(2,128)(2,1)S(1)}, u32[]{:S(2)}, u32[]{:S(2)}) collective-permute-start(bf16[1,2,2048]{2,1,0:T(2,128)(2,1)S(1)} %get-tuple-element.20), channel_id=1, source_target_pairs={{0,7},{1,8},{2,9},{3,10},{4,11},{5,12},{6,13},{7,14},{8,15},{9,0},... | collective-permute-start | bytes 24584 | tf_op jit(solution)/shard_map/ppermute | solution.py:23
  82.9 0.9 collective-permute-start.9
  83.8 0.6 collective-permute-start.10
  84.4 0.4 collective-permute-start.11
  84.8 4.5 %collective-permute-start.12 = (bf16[1,2,2048]{2,1,0:T(2,128)(2,1)S(1)}, bf16[1,2,2048]{2,1,0:T(2,128)(2,1)S(1)}, u32[]{:S(2)}, u32[]{:S(2)}) collective-permute-start(bf16[1,2,2048]{2,1,0:T(2,128)(2,1)S(1)} %get-tuple-element.16), channel_id=1, source_target_pairs={{0,3},{1,4},{2,5},{3,6},{4,7},{5,8},{6,9},{7,10},{8,11},{9,12},{10... | collective-permute-start | bytes 24584 | tf_op jit(solution)/shard_map/ppermute | solution.py:23
  89.4 0.5 collective-permute-start.13
  89.9 0.2 collective-permute-start.14
  90.1 0.1 collective-permute-done.10
  90.2 0.5 collective-permute-done.12
  90.7 3.6 %collective-permute-done.13 = bf16[1,2,2048]{2,1,0:T(2,128)(2,1)S(1)} collective-permute-done((bf16[1,2,2048]{2,1,0:T(2,128)(2,1)S(1)}, bf16[1,2,2048]{2,1,0:T(2,128)(2,1)S(1)}, u32[]{:S(2)}, u32[]{:S(2)}) %collective-permute-start.13) | collective-permute-done | bytes 8224 | tf_op jit(solution)/shard_map/ppermute | solution.py:23
  94.3 1.4 %collective-permute-done.14 = bf16[1,2,2048]{2,1,0:T(2,128)(2,1)S(1)} collective-permute-done((bf16[1,2,2048]{2,1,0:T(2,128)(2,1)S(1)}, bf16[1,2,2048]{2,1,0:T(2,128)(2,1)S(1)}, u32[]{:S(2)}, u32[]{:S(2)}) %collective-permute-start.14) | collective-permute-done | bytes 8224 | tf_op jit(solution)/shard_map/ppermute | solution.py:23
  95.7 0.3 fusion.57
  96.2 3.1 %fusion.4 = f32[32,768]{1,0:T(8,128)} fusion(bf16[32,2048]{1,0:T(8,128)(2,1)S(1)} %reshape.386, bf16[1,2048,768]{2,1,0:T(8,128)(2,1)} %param.26), kind=kOutput, calls=%fused_computation.6 | convolution fusion | flops 100663296 | bytes 3375104 | tf_op jit(solution)/shard_map/dot_general | solution.py:65
  99.3 3.2 %fusion.6 = bf16[32,2048]{1,0:T(8,128)(2,1)S(1)} fusion(bf16[1,768,2048]{2,1,0:T(8,128)(2,1)S(1)} %copy-done, bf16[32,2048]{1,0:T(8,128)(2,1)S(1)} %reshape.386, bf16[1,2048,768]{2,1,0:T(8,128)(2,1)} %param.27, f32[32,768]{1,0:T(8,128)} %fusion.4), kind=kOutput, calls=%fused_computation.9 | convolution fusion | flops 201539584 | bytes 6651904 | tf_op jit(solution)/shard_map/dot_general | solution.py:69
  102.5 0.8 reshape.387
  103.3 3.5 %all-to-all-start = ((bf16[16,2,2048]{2,1,0:T(2,128)(2,1)}), bf16[16,2,2048]{2,1,0:T(2,128)(2,1)S(1)}, u32[]{:S(2)}, u32[]{:S(2)}) async-start(bf16[16,2,2048]{2,1,0:T(2,128)(2,1)} %reshape.387), calls=%async_computation.1 | async-start | bytes 262144 | tf_op jit(solution)/shard_map/all_to_all | solution.py:256
  106.8 0.1 iota_compare_fusion.3
  106.9 7.3 %all-to-all-done = bf16[16,2,2048]{2,1,0:T(2,128)(2,1)S(1)} async-done(((bf16[16,2,2048]{2,1,0:T(2,128)(2,1)}), bf16[16,2,2048]{2,1,0:T(2,128)(2,1)S(1)}, u32[]{:S(2)}, u32[]{:S(2)}) %all-to-all-start) | async-done | bytes 131104 | tf_op jit(solution)/shard_map/all_to_all | solution.py:256
  114.2 0.1 fusion.9
  114.4 0.7 copy.111
  (76 shorter events, 0.7 us)
Async XLA Ops:
  6.5 92.8 %copy-start = (bf16[1,768,2048]{2,1,0:T(8,128)(2,1)S(1)}, bf16[1,768,2048]{2,1,0:T(8,128)(2,1)}, u32[]{:S(2)}) copy-start(bf16[1,768,2048]{2,1,0:T(8,128)(2,1)} %param.28) | copy-start | bytes 9437188
  6.5 21.5 %copy-start.4 = (f32[2048]{0:T(1024)S(1)}, f32[2048]{0:T(1024)}, u32[]{:S(2)}) copy-start(f32[2048]{0:T(1024)} %param.22) | copy-start | bytes 24580
  6.5 62.4 %reduce-scatter.2.cloned.1.call-start = ((), (), s32[]{:S(2)}) async-start(), calls=%async_computation.2 | async-start | bytes 327680 | tf_op jit(solution)/shard_map/reduce_scatter | solution.py:220
  11.1 27.8 %copy-start.7 = (bf16[8,8,512]{2,1,0:T(8,128)(2,1)S(1)}, bf16[8,8,512]{2,1,0:T(8,128)(2,1)}, u32[]{:S(2)}) copy-start(bf16[8,8,512]{2,1,0:T(8,128)(2,1)} %param.21) | copy-start | bytes 196612
  33.1 12.9 %copy-start.1 = (bf16[512,2048]{1,0:T(8,128)(2,1)S(1)}, bf16[512,2048]{1,0:T(8,128)(2,1)}, u32[]{:S(2)}) copy-start(bf16[512,2048]{1,0:T(8,128)(2,1)} %param.24) | copy-start | bytes 6291460
  39.8 7.5 %copy-start.6 = (s32[8,2]{0,1:T(2,128)S(1)}, s32[8,2]{0,1:T(2,128)}, u32[]{:S(2)}) copy-start(s32[8,2]{0,1:T(2,128)} %param.30) | copy-start | bytes 196
  40.1 28.8 %copy-start.2 = (bf16[8,2,2048]{2,1,0:T(2,128)(2,1)S(1)}, bf16[8,2,2048]{2,1,0:T(2,128)(2,1)}, u32[]{:S(2)}) copy-start(bf16[8,2,2048]{2,1,0:T(2,128)(2,1)} %param.20) | copy-start | bytes 196612
  40.1 29.8 %copy-start.5 = (f32[2048]{0:T(1024)S(1)}, f32[2048]{0:T(1024)}, u32[]{:S(2)}) copy-start(f32[2048]{0:T(1024)} %param.25) | copy-start | bytes 24580
  71.7 5.5 %collective-permute-start = (bf16[1,2,2048]{2,1,0:T(2,128)(2,1)S(1)}, bf16[1,2,2048]{2,1,0:T(2,128)(2,1)S(1)}, u32[]{:S(2)}, u32[]{:S(2)}) collective-permute-start(bf16[1,2,2048]{2,1,0:T(2,128)(2,1)S(1)} %get-tuple-element.28), channel_id=1, source_target_pairs={{0,15},{1,0},{2,1},{3,2},{4,3},{5,4},{6,5},{7,6},{8,7},{9,8},{10,9... | collective-permute-start | bytes 24584 | tf_op jit(solution)/shard_map/ppermute | solution.py:23
  71.8 6.7 %collective-permute-start.1 = (bf16[1,2,2048]{2,1,0:T(2,128)(2,1)S(1)}, bf16[1,2,2048]{2,1,0:T(2,128)(2,1)S(1)}, u32[]{:S(2)}, u32[]{:S(2)}) collective-permute-start(bf16[1,2,2048]{2,1,0:T(2,128)(2,1)S(1)} %get-tuple-element.27), channel_id=1, source_target_pairs={{0,14},{1,15},{2,0},{3,1},{4,2},{5,3},{6,4},{7,5},{8,6},{9,7},{10,... | collective-permute-start | bytes 24584 | tf_op jit(solution)/shard_map/ppermute | solution.py:23
  71.9 8.5 %collective-permute-start.2 = (bf16[1,2,2048]{2,1,0:T(2,128)(2,1)S(1)}, bf16[1,2,2048]{2,1,0:T(2,128)(2,1)S(1)}, u32[]{:S(2)}, u32[]{:S(2)}) collective-permute-start(bf16[1,2,2048]{2,1,0:T(2,128)(2,1)S(1)} %get-tuple-element.26), channel_id=1, source_target_pairs={{0,13},{1,14},{2,15},{3,0},{4,1},{5,2},{6,3},{7,4},{8,5},{9,6},{10... | collective-permute-start | bytes 24584 | tf_op jit(solution)/shard_map/ppermute | solution.py:23
  75.0 6.0 %collective-permute-start.3 = (bf16[1,2,2048]{2,1,0:T(2,128)(2,1)S(1)}, bf16[1,2,2048]{2,1,0:T(2,128)(2,1)S(1)}, u32[]{:S(2)}, u32[]{:S(2)}) collective-permute-start(bf16[1,2,2048]{2,1,0:T(2,128)(2,1)S(1)} %get-tuple-element.25), channel_id=1, source_target_pairs={{0,12},{1,13},{2,14},{3,15},{4,0},{5,1},{6,2},{7,3},{8,4},{9,5},{1... | collective-permute-start | bytes 24584 | tf_op jit(solution)/shard_map/ppermute | solution.py:23
  75.1 7.8 %collective-permute-start.4 = (bf16[1,2,2048]{2,1,0:T(2,128)(2,1)S(1)}, bf16[1,2,2048]{2,1,0:T(2,128)(2,1)S(1)}, u32[]{:S(2)}, u32[]{:S(2)}) collective-permute-start(bf16[1,2,2048]{2,1,0:T(2,128)(2,1)S(1)} %get-tuple-element.24), channel_id=1, source_target_pairs={{0,11},{1,12},{2,13},{3,14},{4,15},{5,0},{6,1},{7,2},{8,3},{9,4},{... | collective-permute-start | bytes 24584 | tf_op jit(solution)/shard_map/ppermute | solution.py:23
  77.2 6.5 %collective-permute-start.5 = (bf16[1,2,2048]{2,1,0:T(2,128)(2,1)S(1)}, bf16[1,2,2048]{2,1,0:T(2,128)(2,1)S(1)}, u32[]{:S(2)}, u32[]{:S(2)}) collective-permute-start(bf16[1,2,2048]{2,1,0:T(2,128)(2,1)S(1)} %get-tuple-element.23), channel_id=1, source_target_pairs={{0,10},{1,11},{2,12},{3,13},{4,14},{5,15},{6,0},{7,1},{8,2},{9,3},... | collective-permute-start | bytes 24584 | tf_op jit(solution)/shard_map/ppermute | solution.py:23
  78.5 5.9 %collective-permute-start.6 = (bf16[1,2,2048]{2,1,0:T(2,128)(2,1)S(1)}, bf16[1,2,2048]{2,1,0:T(2,128)(2,1)S(1)}, u32[]{:S(2)}, u32[]{:S(2)}) collective-permute-start(bf16[1,2,2048]{2,1,0:T(2,128)(2,1)S(1)} %get-tuple-element.22), channel_id=1, source_target_pairs={{0,9},{1,10},{2,11},{3,12},{4,13},{5,14},{6,15},{7,0},{8,1},{9,2},... | collective-permute-start | bytes 24584 | tf_op jit(solution)/shard_map/ppermute | solution.py:23
  80.4 4.5 %collective-permute-start.7 = (bf16[1,2,2048]{2,1,0:T(2,128)(2,1)S(1)}, bf16[1,2,2048]{2,1,0:T(2,128)(2,1)S(1)}, u32[]{:S(2)}, u32[]{:S(2)}) collective-permute-start(bf16[1,2,2048]{2,1,0:T(2,128)(2,1)S(1)} %get-tuple-element.21), channel_id=1, source_target_pairs={{0,8},{1,9},{2,10},{3,11},{4,12},{5,13},{6,14},{7,15},{8,0},{9,1},... | collective-permute-start | bytes 24584 | tf_op jit(solution)/shard_map/ppermute | solution.py:23
  81.0 8.3 %collective-permute-start.8 = (bf16[1,2,2048]{2,1,0:T(2,128)(2,1)S(1)}, bf16[1,2,2048]{2,1,0:T(2,128)(2,1)S(1)}, u32[]{:S(2)}, u32[]{:S(2)}) collective-permute-start(bf16[1,2,2048]{2,1,0:T(2,128)(2,1)S(1)} %get-tuple-element.20), channel_id=1, source_target_pairs={{0,7},{1,8},{2,9},{3,10},{4,11},{5,12},{6,13},{7,14},{8,15},{9,0},... | collective-permute-start | bytes 24584 | tf_op jit(solution)/shard_map/ppermute | solution.py:23
  82.9 7.0 %collective-permute-start.9 = (bf16[1,2,2048]{2,1,0:T(2,128)(2,1)S(1)}, bf16[1,2,2048]{2,1,0:T(2,128)(2,1)S(1)}, u32[]{:S(2)}, u32[]{:S(2)}) collective-permute-start(bf16[1,2,2048]{2,1,0:T(2,128)(2,1)S(1)} %get-tuple-element.19), channel_id=1, source_target_pairs={{0,6},{1,7},{2,8},{3,9},{4,10},{5,11},{6,12},{7,13},{8,14},{9,15},... | collective-permute-start | bytes 24584 | tf_op jit(solution)/shard_map/ppermute | solution.py:23
  83.8 6.4 %collective-permute-start.10 = (bf16[1,2,2048]{2,1,0:T(2,128)(2,1)S(1)}, bf16[1,2,2048]{2,1,0:T(2,128)(2,1)S(1)}, u32[]{:S(2)}, u32[]{:S(2)}) collective-permute-start(bf16[1,2,2048]{2,1,0:T(2,128)(2,1)S(1)} %get-tuple-element.18), channel_id=1, source_target_pairs={{0,5},{1,6},{2,7},{3,8},{4,9},{5,10},{6,11},{7,12},{8,13},{9,14},{... | collective-permute-start | bytes 24584 | tf_op jit(solution)/shard_map/ppermute | solution.py:23
  84.4 5.8 %collective-permute-start.11 = (bf16[1,2,2048]{2,1,0:T(2,128)(2,1)S(1)}, bf16[1,2,2048]{2,1,0:T(2,128)(2,1)S(1)}, u32[]{:S(2)}, u32[]{:S(2)}) collective-permute-start(bf16[1,2,2048]{2,1,0:T(2,128)(2,1)S(1)} %get-tuple-element.17), channel_id=1, source_target_pairs={{0,4},{1,5},{2,6},{3,7},{4,8},{5,9},{6,10},{7,11},{8,12},{9,13},{1... | collective-permute-start | bytes 24584 | tf_op jit(solution)/shard_map/ppermute | solution.py:23
  84.8 5.9 %collective-permute-start.12 = (bf16[1,2,2048]{2,1,0:T(2,128)(2,1)S(1)}, bf16[1,2,2048]{2,1,0:T(2,128)(2,1)S(1)}, u32[]{:S(2)}, u32[]{:S(2)}) collective-permute-start(bf16[1,2,2048]{2,1,0:T(2,128)(2,1)S(1)} %get-tuple-element.16), channel_id=1, source_target_pairs={{0,3},{1,4},{2,5},{3,6},{4,7},{5,8},{6,9},{7,10},{8,11},{9,12},{10... | collective-permute-start | bytes 24584 | tf_op jit(solution)/shard_map/ppermute | solution.py:23
  89.4 4.9 %collective-permute-start.13 = (bf16[1,2,2048]{2,1,0:T(2,128)(2,1)S(1)}, bf16[1,2,2048]{2,1,0:T(2,128)(2,1)S(1)}, u32[]{:S(2)}, u32[]{:S(2)}) collective-permute-start(bf16[1,2,2048]{2,1,0:T(2,128)(2,1)S(1)} %get-tuple-element.15), channel_id=1, source_target_pairs={{0,2},{1,3},{2,4},{3,5},{4,6},{5,7},{6,8},{7,9},{8,10},{9,11},{10,... | collective-permute-start | bytes 24584 | tf_op jit(solution)/shard_map/ppermute | solution.py:23
  89.9 5.8 %collective-permute-start.14 = (bf16[1,2,2048]{2,1,0:T(2,128)(2,1)S(1)}, bf16[1,2,2048]{2,1,0:T(2,128)(2,1)S(1)}, u32[]{:S(2)}, u32[]{:S(2)}) collective-permute-start(bf16[1,2,2048]{2,1,0:T(2,128)(2,1)S(1)} %get-tuple-element.14), channel_id=1, source_target_pairs={{0,1},{1,2},{2,3},{3,4},{4,5},{5,6},{6,7},{7,8},{8,9},{9,10},{10,1... | collective-permute-start | bytes 24584 | tf_op jit(solution)/shard_map/ppermute | solution.py:23
  99.3 14.9 %copy-start.3 = (bf16[2,8,2048]{2,1,0:T(8,128)(2,1)S(1)}, bf16[2,8,2048]{2,1,0:T(8,128)(2,1)}, u32[]{:S(2)}) copy-start(bf16[2,8,2048]{2,1,0:T(8,128)(2,1)} %reduce-scatter.2.cloned.1.call-done) | copy-start | bytes 196612
  103.3 10.9 %all-to-all-start = ((bf16[16,2,2048]{2,1,0:T(2,128)(2,1)}), bf16[16,2,2048]{2,1,0:T(2,128)(2,1)S(1)}, u32[]{:S(2)}, u32[]{:S(2)}) async-start(bf16[16,2,2048]{2,1,0:T(2,128)(2,1)} %reshape.387), calls=%async_computation.1 | async-start | bytes 262144 | tf_op jit(solution)/shard_map/all_to_all | solution.py:256
Sparse Core Ops, SparseCore 0:
  47.4 21.5 reduce-scatter.1
